TPU v7x, 32 devices: a whole 2x2x4 slice. The times are simulated.
32 devices in a mesh: seq: 4 (over y, core), head: 8 (over z, x).
Axes of the slice: x: 2, y: 2, z: 4, core: 2. Of those that a mesh axis runs over, the one named last changes fastest.
Arguments:
- queries: bfloat16 [8, 2048, 256], P('head', 'seq'), may hold values from -6 to 6
- keys: bfloat16 [1, 2048, 256], P(None, 'seq'), may hold values from -6 to 6
- values: bfloat16 [1, 2048, 256], P(None, 'seq'), may hold values from -6 to 6
- d_out: bfloat16 [8, 2048, 256], P('head', 'seq'), may hold values from -12 to 12
- doc_lengths: int32 [1, 8], replicated, may hold values from 1 to 768, 2048 in all within a row
- fold_order: int32 [8], replicated, may hold values from 0 to 7, each once
Outputs:
- grad_queries: bfloat16 [8, 2048, 256], P('head', 'seq')
- grad_keys: float32 [1, 2048, 256], P(None, ('seq', 'head'))
- grad_values: float32 [1, 2048, 256], P(None, ('seq', 'head'))
Inputs may be any that keep to these rules, and one draw needn't show every extreme that they name: `doc_lengths`: each row's 8 lengths are at least 1, sum to 2048, and the longest is exactly 768. fold_order names each of 0 to 7 once.
All inputs are finite; a program needn't handle non-finite values.
Results may differ from a plain program's by a relative error of at most 0.029.
Values may be sent and summed in bfloat16 or wider, within the bound.
No kernel may reach another device: no remote copies, remote signals or barrier semaphores. Data moves between devices by JAX's collectives and lax.ppermute only.
A program may use at most 64 MiB of HBM per device.

v0:
```python
import jax
import jax.numpy as jnp
from jax import lax
from jax.sharding import PartitionSpec as P

HEAD_COUNT = 8
masked_value = -1e30


def contract_last(left, right):
    return lax.dot_general(
        left, right, (((1,), (1,)), ((), ())), preferred_element_type=jnp.float32
    )


def contract_first(left, right):
    return lax.dot_general(
        left, right, (((0,), (0,)), ((), ())), preferred_element_type=jnp.float32
    )


def block_grads(query_rows, grad_out, log_norm, grad_dot, key_part, value_part, allowed, scaling):
    scores = contract_last(query_rows, key_part) * scaling
    weights = jnp.exp(jnp.where(allowed, scores - log_norm, masked_value))
    weights_low = weights.astype(jnp.bfloat16)
    grad_prob = contract_last(grad_out, value_part)
    grad_score = (weights * (grad_prob - grad_dot)).astype(jnp.bfloat16)
    part_query = jnp.dot(grad_score, key_part, preferred_element_type=jnp.float32) * scaling
    part_key = contract_first(grad_score, query_rows) * scaling
    part_value = contract_first(weights_low, grad_out)
    return (part_query, part_key, part_value)


def owner_blocks(key_part, value_part, row_count):
    head_total = lax.axis_size("head")
    piece_len = key_part.shape[0] // head_total
    width = key_part.shape[1]
    moved = (
        lax.all_to_all(
            key_part.astype(jnp.bfloat16), "head", split_axis=0, concat_axis=0, tiled=True
        ).astype(key_part.dtype),
        lax.all_to_all(
            value_part.astype(jnp.bfloat16), "head", split_axis=0, concat_axis=0, tiled=True
        ).astype(value_part.dtype),
    )
    return tuple(
        (
            jnp.sum(item.reshape(row_count, head_total // row_count, piece_len, width), axis=1)
            for item in moved
        )
    )


def per_device(queries, keys, values, d_out, doc_lengths, fold_order):
    local_len = queries.shape[1]
    head_width = queries.shape[2]
    half_len = local_len // 2
    scaling = head_width ** (-0.5)
    seq_index = lax.axis_index("seq")
    row_index = lax.axis_index("head") // HEAD_COUNT
    row_count = keys.shape[0]
    span_ids = jnp.arange(fold_order.shape[0], dtype=jnp.int32)
    lengths = lax.dynamic_index_in_dim(doc_lengths, row_index, 0, keepdims=False)
    starts = jnp.cumsum(lengths, dtype=jnp.int32) - lengths

    def locate(indices):
        block_of = indices // half_len
        anchor = jnp.sum(
            jnp.where(block_of[:, None] == span_ids[None, :], fold_order[None, :], 0),
            axis=1,
            dtype=jnp.int32,
        )
        position = anchor * half_len + indices % half_len
        document = jnp.sum(
            (position[:, None] >= starts[None, :]).astype(jnp.int32), axis=1, dtype=jnp.int32
        )
        return (position, document)

    def allowed_pairs(query_place, key_place):
        return (query_place[1][:, None] == key_place[1][None, :]) & (
            key_place[0][None, :] <= query_place[0][:, None]
        )

    local_rows = jnp.arange(local_len, dtype=jnp.int32)
    own_place = locate(seq_index * local_len + local_rows)
    query_rows = queries[0]
    grad_out = d_out[0]
    key_row = lax.dynamic_index_in_dim(keys, row_index, 0, keepdims=False)
    value_row = lax.dynamic_index_in_dim(values, row_index, 0, keepdims=False)
    key_part = lax.all_gather(key_row, "seq", axis=0, tiled=True)
    value_part = lax.all_gather(value_row, "seq", axis=0, tiled=True)
    allowed = allowed_pairs(own_place, locate(jnp.arange(key_part.shape[0], dtype=jnp.int32)))
    run_max = jnp.full((local_len, 1), masked_value, jnp.float32)
    scores = jnp.where(allowed, contract_last(query_rows, key_part) * scaling, masked_value)
    new_max = jnp.maximum(run_max, jnp.max(scores, axis=1, keepdims=True))
    weights = jnp.where(allowed, jnp.exp(scores - new_max), 0.0)
    sum_next = jnp.sum(weights, axis=1, keepdims=True)
    acc_next = jnp.dot(weights.astype(jnp.bfloat16), value_part, preferred_element_type=jnp.float32)
    log_norm = new_max + jnp.log(sum_next)
    output = acc_next / sum_next
    grad_dot = jnp.sum(grad_out.astype(jnp.float32) * output, axis=1, keepdims=True)
    key_part = lax.all_gather(key_row, "seq", axis=0, tiled=True)
    value_part = lax.all_gather(value_row, "seq", axis=0, tiled=True)
    row_total = key_part.shape[0]
    allowed = allowed_pairs(own_place, locate(jnp.arange(row_total, dtype=jnp.int32)))
    part_query, part_key, part_value = block_grads(
        query_rows, grad_out, log_norm, grad_dot, key_part, value_part, allowed, scaling
    )
    full_keys = part_key
    full_values = part_value
    grad_query, full_keys, full_values = (part_query, full_keys, full_values)
    seq_keys, seq_values = (
        lax.psum_scatter(
            full_keys.astype(jnp.bfloat16), "seq", scatter_dimension=0, tiled=True
        ).astype(jnp.float32),
        lax.psum_scatter(
            full_values.astype(jnp.bfloat16), "seq", scatter_dimension=0, tiled=True
        ).astype(jnp.float32),
    )
    grad_keys, grad_values = owner_blocks(seq_keys, seq_values, row_count)
    grad_queries = grad_query.astype(jnp.bfloat16)[None]
    return (grad_queries, grad_keys, grad_values)


def solution(mesh):
    in_specs = (
        P("head", "seq", None),
        P(None, "seq", None),
        P(None, "seq", None),
        P("head", "seq", None),
        P(),
        P(),
    )
    out_specs = (
        P("head", "seq", None),
        P(None, ("seq", "head"), None),
        P(None, ("seq", "head"), None),
    )
    return jax.shard_map(
        per_device, mesh=mesh, in_specs=in_specs, out_specs=out_specs, check_vma=False
    )
```

profile of v0, /device:TPU:0, one launch (start us, length us, event | category | flops | bytes accessed | tf_op | source)
XLA Modules:
  0.0 123.3 jit_solution(2231959383606064671)
XLA Ops:
  7.2 0.0 copy-start
  7.2 0.0 all-gather.5.cloned.1.call-start
  7.2 0.7 all-gather.5.cloned.1.call-update
  7.9 0.0 all-gather.7.cloned.1.call-start
  8.0 0.7 all-gather.7.cloned.1.call-update
  8.7 0.0 reduce-scatter.5.cloned.1.call-start
  8.7 0.8 reduce-window_clone.1
  9.6 0.7 subtract_bitcast_fusion
  10.2 0.7 select_reduce_fusion.1
  11.0 0.7 select_reduce_fusion
  11.7 0.1 convert_reduce_fusion.3
  11.8 0.1 convert_reduce_fusion.2
  11.9 17.1 %all-gather.5.cloned.1.call-done = bf16[1,2048,256]{2,1,0:T(8,128)(2,1)} async-done(((bf16[1,512,256]{2,1,0:T(8,128)(2,1)}), bf16[1,2048,256]{2,1,0:T(8,128)(2,1)}) %all-gather.5.cloned.1.call-update) | async-done | bytes 1048592 | tf_op jit(solution)/shard_map/all_gather | solution.py:102
  29.0 0.0 copy-done
  29.0 2.6 %fusion = (f32[512]{0:T(512)S(1)}, f32[512,2048]{1,0:T(8,128)S(1)}) fusion(s32[512]{0:T(512)S(1)} %fusion.45, s32[2048]{0:T(1024)S(1)} %fusion.43, s32[2048]{0:T(1024)S(1)} %convert_reduce_fusion.2, s32[512]{0:T(512)S(1)} %convert_reduce_fusion.3, bf16[1,2048,256]{2,1,0:T(8,128)(2,1)} %all-gather.5.cloned.1.call-done, bf16[1,512,256]{2,1,0:T(8,128)(2,1)S(1)} %copy-done), kind=kOutput, calls=%fused_computation.5 | convolution fusion | flops 543161856 | bytes 5527552 | tf_op jit(solution)/shard_map/dot_general | solution.py:11
  31.6 0.0 copy-start.1
  31.6 0.0 copy-start.3
  31.6 1.7 %fusion.4 = f32[512]{0:T(512)S(1)} fusion(f32[512,2048]{1,0:T(8,128)S(1)} %get-tuple-element.4, f32[512]{0:T(512)S(1)} %broadcast_maximum_fusion, s32[512]{0:T(512)S(1)} %fusion.45, s32[2048]{0:T(1024)S(1)} %fusion.43, s32[2048]{0:T(1024)S(1)} %convert_reduce_fusion.2, s32[512]{0:T(512)S(1)} %convert_reduce_fusion.3), kind=kLoop, calls=%fused_computation.11 | loop fusion | flops 8388096 | bytes 4218880 | tf_op jit(solution)/shard_map/reduce_sum | solution.py:97
  33.3 0.2 copy-done.1
  33.5 0.0 copy-done.3
  33.5 2.9 %convolution_convert_fusion = bf16[2048,256]{1,0:T(8,128)(2,1)} fusion(f32[512,2048]{1,0:T(8,128)S(1)} %get-tuple-element.4, f32[512]{0:T(512)S(1)} %log_add_fusion, bf16[1,512,256]{2,1,0:T(8,128)(2,1)S(1)} %copy-done.3, s32[2048]{0:T(1024)S(1)} %fusion.43, s32[2048]{0:T(1024)S(1)} %convert_reduce_fusion.2, s32[512]{0:T(512)S(1)} %fusion.45, ...), kind=kOutput, calls=%fused_computation.9 | convolution fusion | flops 544735232 | bytes 5527552 | tf_op jit(solution)/shard_map/dot_general | solution.py:17
  36.4 0.0 reduce-scatter.5.cloned.1.call-update
  36.5 0.0 reduce-scatter.3.cloned.1.call-start
  36.5 0.1 copy.10
  36.7 10.6 %all-gather.7.cloned.1.call-done = bf16[1,2048,256]{2,1,0:T(8,128)(2,1)} async-done(((bf16[1,512,256]{2,1,0:T(8,128)(2,1)}), bf16[1,2048,256]{2,1,0:T(8,128)(2,1)}) %all-gather.7.cloned.1.call-update) | async-done | bytes 1048592 | tf_op jit(solution)/shard_map/all_gather | solution.py:103
  47.3 0.0 copy-start.2
  47.3 0.0 copy-start.5
  47.3 4.2 %fusion.28 = f32[512]{0:T(512)S(1)} fusion(bf16[1,2048,256]{2,1,0:T(8,128)(2,1)} %all-gather.7.cloned.1.call-done, f32[512,2048]{1,0:T(8,128)} %copy-done.1, f32[512]{0:T(512)S(1)} %broadcast_maximum_fusion, bf16[1,512,256]{1,2,0:T(8,128)(2,1)S(1)} %copy.10, f32[512]{0:T(512)S(1)} %fusion.4, s32[2048]{0:T(1024)S(1)} %fusion.43, ...), kind=kOutput, calls=%fused_computation.26 | convolution fusion | flops 545783296 | bytes 5531648 | tf_op jit(solution)/shard_map/dot_general | solution.py:98
  51.5 0.0 copy-done.2
  51.5 0.0 copy-done.5
  51.5 2.1 %multiply_convert_fusion = bf16[512,2048]{1,0:T(8,128)(2,1)S(1)} fusion(f32[512,2048]{1,0:T(8,128)S(1)} %copy-done.2, f32[512]{0:T(512)S(1)} %fusion.28, f32[512]{0:T(512)S(1)} %log_add_fusion, bf16[1,2048,256]{2,1,0:T(8,128)(2,1)S(1)} %copy-done.5, bf16[1,512,256]{2,1,0:T(8,128)(2,1)S(1)} %copy-done.3, s32[512]{0:T(512)S(1)} %fusion.45, ...), kind=kOutput, calls=%fused_computation | convolution fusion | flops 546308096 | bytes 7626752 | tf_op jit(solution)/shard_map/dot_general | solution.py:11
  53.6 0.0 copy-start.6
  53.6 1.3 %copy-done.6 = bf16[512,2048]{1,0:T(8,128)(2,1)} copy-done((bf16[512,2048]{1,0:T(8,128)(2,1)}, bf16[512,2048]{1,0:T(8,128)(2,1)S(1)}, u32[]{:S(2)}) %copy-start.6) | copy-done | bytes 2097176
  54.9 0.0 copy-start.4
  54.9 1.8 %fusion.2 = bf16[2048,256]{1,0:T(8,128)(2,1)} fusion(bf16[512,2048]{1,0:T(8,128)(2,1)S(1)} %multiply_convert_fusion, bf16[1,512,256]{2,1,0:T(8,128)(2,1)S(1)} %copy-done), kind=kOutput, calls=%fused_computation.8 | convolution fusion | flops 537919488 | bytes 3407872 | tf_op jit(solution)/shard_map/dot_general | solution.py:17
  56.7 0.0 reduce-scatter.3.cloned.1.call-update
  56.7 17.9 %reduce-scatter.5.cloned.1.call-done = bf16[512,256]{1,0:T(8,128)(2,1)} async-done(((bf16[2048,256]{1,0:T(8,128)(2,1)}), bf16[512,256]{1,0:T(8,128)(2,1)}) %reduce-scatter.5.cloned.1.call-update) | async-done | bytes 262160 | tf_op jit(solution)/shard_map/reduce_scatter | solution.py:116
  74.7 5.5 %all-to-all-start.1 = ((bf16[8,64,256]{2,1,0:T(8,128)(2,1)}), bf16[8,64,256]{2,1,0:T(8,128)(2,1)S(1)}, u32[]{:S(2)}, u32[]{:S(2)}) async-start(bf16[8,64,256]{2,1,0:T(8,128)(2,1)} %bitcast.43), calls=%async_computation.3 | async-start | bytes 524288 | tf_op jit(solution)/shard_map/all_to_all | solution.py:42
  80.2 21.7 %reduce-scatter.3.cloned.1.call-done = bf16[512,256]{1,0:T(8,128)(2,1)} async-done(((bf16[2048,256]{1,0:T(8,128)(2,1)}), bf16[512,256]{1,0:T(8,128)(2,1)}) %reduce-scatter.3.cloned.1.call-update) | async-done | bytes 262160 | tf_op jit(solution)/shard_map/reduce_scatter | solution.py:113
  101.9 0.0 all-to-all-done.1
  101.9 5.5 %all-to-all-start = ((bf16[8,64,256]{2,1,0:T(8,128)(2,1)}), bf16[8,64,256]{2,1,0:T(8,128)(2,1)S(1)}, u32[]{:S(2)}, u32[]{:S(2)}) async-start(bf16[8,64,256]{2,1,0:T(8,128)(2,1)} %bitcast.44), calls=%async_computation.1 | async-start | bytes 524288 | tf_op jit(solution)/shard_map/all_to_all | solution.py:39
  107.4 0.0 copy-done.4
  107.4 3.0 %fusion.12 = bf16[1,512,256]{2,1,0:T(8,128)(2,1)} fusion(bf16[512,2048]{1,0:T(8,128)(2,1)} %copy-done.6, bf16[1,2048,256]{2,1,0:T(8,128)(2,1)S(1)} %copy-done.4), kind=kOutput, calls=%fused_computation.18 | convolution fusion | flops 537133056 | bytes 3407872 | tf_op jit(solution)/shard_map/dot_general | solution.py:28
  110.4 0.7 convert_reduce_fusion
  111.1 5.1 %all-to-all-done = bf16[8,64,256]{2,1,0:T(8,128)(2,1)S(1)} async-done(((bf16[8,64,256]{2,1,0:T(8,128)(2,1)}), bf16[8,64,256]{2,1,0:T(8,128)(2,1)S(1)}, u32[]{:S(2)}, u32[]{:S(2)}) %all-to-all-start) | async-done | bytes 262176 | tf_op jit(solution)/shard_map/all_to_all | solution.py:39
  116.1 0.7 convert_reduce_fusion.1
  (6 shorter events, 0.0 us)
Async XLA Ops:
  7.2 21.8 %copy-start = (bf16[1,512,256]{2,1,0:T(8,128)(2,1)S(1)}, bf16[1,512,256]{2,1,0:T(8,128)(2,1)}, u32[]{:S(2)}) copy-start(bf16[1,512,256]{2,1,0:T(8,128)(2,1)} %param.6) | copy-start | bytes 786436
  7.2 21.8 %all-gather.5.cloned.1.call-start = ((), (), s32[]{:S(2)}) async-start(), calls=%async_computation.6 | async-start | bytes 1310720 | tf_op jit(solution)/shard_map/all_gather | solution.py:102
  7.9 39.4 %all-gather.7.cloned.1.call-start = ((), (), s32[]{:S(2)}) async-start(), calls=%async_computation.7 | async-start | bytes 1310720 | tf_op jit(solution)/shard_map/all_gather | solution.py:103
  8.7 66.0 %reduce-scatter.5.cloned.1.call-start = ((), (), s32[]{:S(2)}) async-start(), calls=%async_computation.5 | async-start | bytes 1310720 | tf_op jit(solution)/shard_map/reduce_scatter | solution.py:116
  31.6 1.9 %copy-start.1 = (f32[512,2048]{1,0:T(8,128)}, f32[512,2048]{1,0:T(8,128)S(1)}, u32[]{:S(2)}) copy-start(f32[512,2048]{1,0:T(8,128)S(1)} %get-tuple-element.4) | copy-start | bytes 12582916
  31.6 1.9 %copy-start.3 = (bf16[1,512,256]{2,1,0:T(8,128)(2,1)S(1)}, bf16[1,512,256]{2,1,0:T(8,128)(2,1)}, u32[]{:S(2)}) copy-start(bf16[1,512,256]{2,1,0:T(8,128)(2,1)} %param.9) | copy-start | bytes 786436
  36.5 65.4 %reduce-scatter.3.cloned.1.call-start = ((), (), s32[]{:S(2)}) async-start(), calls=%async_computation.4 | async-start | bytes 1310720 | tf_op jit(solution)/shard_map/reduce_scatter | solution.py:113
  47.3 4.2 %copy-start.2 = (f32[512,2048]{1,0:T(8,128)S(1)}, f32[512,2048]{1,0:T(8,128)}, u32[]{:S(2)}) copy-start(f32[512,2048]{1,0:T(8,128)} %copy-done.1) | copy-start | bytes 12582916
  47.3 4.2 %copy-start.5 = (bf16[1,2048,256]{2,1,0:T(8,128)(2,1)S(1)}, bf16[1,2048,256]{2,1,0:T(8,128)(2,1)}, u32[]{:S(2)}) copy-start(bf16[1,2048,256]{2,1,0:T(8,128)(2,1)} %all-gather.7.cloned.1.call-done) | copy-start | bytes 3145732
  53.6 1.4 %copy-start.6 = (bf16[512,2048]{1,0:T(8,128)(2,1)}, bf16[512,2048]{1,0:T(8,128)(2,1)S(1)}, u32[]{:S(2)}) copy-start(bf16[512,2048]{1,0:T(8,128)(2,1)S(1)} %multiply_convert_fusion) | copy-start | bytes 6291460
  54.9 52.4 %copy-start.4 = (bf16[1,2048,256]{2,1,0:T(8,128)(2,1)S(1)}, bf16[1,2048,256]{2,1,0:T(8,128)(2,1)}, u32[]{:S(2)}) copy-start(bf16[1,2048,256]{2,1,0:T(8,128)(2,1)} %all-gather.5.cloned.1.call-done) | copy-start | bytes 3145732
  74.7 27.2 %all-to-all-start.1 = ((bf16[8,64,256]{2,1,0:T(8,128)(2,1)}), bf16[8,64,256]{2,1,0:T(8,128)(2,1)S(1)}, u32[]{:S(2)}, u32[]{:S(2)}) async-start(bf16[8,64,256]{2,1,0:T(8,128)(2,1)} %bitcast.43), calls=%async_computation.3 | async-start | bytes 524288 | tf_op jit(solution)/shard_map/all_to_all | solution.py:42
  101.9 14.3 %all-to-all-start = ((bf16[8,64,256]{2,1,0:T(8,128)(2,1)}), bf16[8,64,256]{2,1,0:T(8,128)(2,1)S(1)}, u32[]{:S(2)}, u32[]{:S(2)}) async-start(bf16[8,64,256]{2,1,0:T(8,128)(2,1)} %bitcast.44), calls=%async_computation.1 | async-start | bytes 524288 | tf_op jit(solution)/shard_map/all_to_all | solution.py:39
Sparse Core Ops, SparseCore 0:
  9.5 19.4 all-gather.4
  30.6 16.6 all-gather.6
  49.8 24.7 reduce-scatter.4
  77.0 24.7 reduce-scatter.2
where the time goes:
time: 124 us; the launch traced here: 123 us
  waiting for transfers between devices  73.8 us (60%)
  matrix products  16.5 us (13%)
  between operations  13.9 us (11%)
  starting transfers between devices  11.2 us (9%)
  other arithmetic  6.24 us (5%)
  local copies, waits for them, and re-layouts  1.69 us (1%)
    reduce_scatter x1, waiting for transfers between devices, per_device(): lax.psum_scatter(full_keys.astype(jnp.bfloat16), 'seq', scatter_dimension...  21.7 us
    reduce_scatter x1, waiting for transfers between devices, per_device(): lax.psum_scatter(full_values.astype(jnp.bfloat16), 'seq', scatter_dimensi...  17.9 us
    all_gather x1, waiting for transfers between devices, per_device(): key_part = lax.all_gather(key_row, 'seq', axis=0, tiled=True)  17.1 us
    all_gather x1, waiting for transfers between devices, per_device(): value_part = lax.all_gather(value_row, 'seq', axis=0, tiled=True)  10.6 us
    all_to_all x1, starting transfers between devices, owner_blocks(): lax.all_to_all(value_part.astype(jnp.bfloat16), 'head', split_axis=0, con...  5.51 us
    all_to_all x1, starting transfers between devices, owner_blocks(): lax.all_to_all(key_part.astype(jnp.bfloat16), 'head', split_axis=0, conca...  5.51 us
    all_to_all x1, waiting for transfers between devices, owner_blocks(): lax.all_to_all(key_part.astype(jnp.bfloat16), 'head', split_axis=0, conca...  5.07 us
    dot_general x2, matrix products, contract_first(): lax.dot_general(left, right, (((0,), (0,)), ((), ())), preferred_element_...  4.69 us
  transfers between devices with their start and end apart: 6, of which 5 were waited for; matrix products, arithmetic and copies ran while one was open for 18% of the time, Pallas kernels for 0%

commit v1 on v0

--- a/solution.py
+++ b/solution.py
@@ -100,7 +100,12 @@
     output = acc_next / sum_next
     grad_dot = jnp.sum(grad_out.astype(jnp.float32) * output, axis=1, keepdims=True)
     key_part = lax.all_gather(key_row, "seq", axis=0, tiled=True)
-    value_part = lax.all_gather(value_row, "seq", axis=0, tiled=True)
+    ring = [value_row]
+    for hop in range(3):
+        ring.append(lax.ppermute(ring[-1], "seq", [(dev, (dev + 1) % 4) for dev in range(4)]))
+    value_part = jnp.roll(
+        jnp.concatenate(ring[::-1], axis=0), (lax.axis_index("seq") + 1) * ring[0].shape[0], axis=0
+    )
     row_total = key_part.shape[0]
     allowed = allowed_pairs(own_place, locate(jnp.arange(row_total, dtype=jnp.int32)))
     part_query, part_key, part_value = block_grads(

time: 124 us -> 125 us (level)
  waiting for transfers between devices: 73.8 us -> 64.1 us
  local copies, waits for them, and re-layouts: 1.69 us -> 8.44 us
  starting transfers between devices: 11.2 us -> 14.3 us
  matrix products: 16.5 us -> 17.8 us
    all_gather x1, waiting for transfers between devices: 17.1 us -> 0.01 us  [per_device(): key_part = lax.all_gather(key_row, 'seq', axis=0, tiled=True)]
    ppermute x0 -> x3, waiting for transfers between devices: none -> 14.2 us  [per_device(): lax.ppermute(ring[-1], 'seq', [(dev, (dev + 1) % 4) for dev in range(4)])]
    unnamed x15 -> x22, local copies, waits for them, and re-layouts: 1.69 us -> 7.71 us
    all_gather x1, waiting for transfers between devices: 10.6 us -> 4.99 us  [per_device(): value_part = lax.all_gather(value_row, 'seq', axis=0, tiled=True)]
    ppermute x0 -> x3, starting transfers between devices: none -> 3.13 us  [per_device(): lax.ppermute(ring[-1], 'seq', [(dev, (dev + 1) % 4) for dev in range(4)])]
  transfers between devices with their start and end apart: 6 -> 9, of which waited for: 5 -> 7; matrix products, arithmetic and copies ran while one was open for 18% -> 24% of each run, Pallas kernels for 0% -> 0%
where the time goes in v1:
time: 125 us
  waiting for transfers between devices  64.1 us (51%)
  matrix products  17.8 us (14%)
  starting transfers between devices  14.3 us (11%)
  between operations  13.9 us (11%)
  local copies, waits for them, and re-layouts  8.44 us (7%)
  other arithmetic  6.24 us (5%)
    reduce_scatter x1, waiting for transfers between devices, per_device(): lax.psum_scatter(full_keys.astype(jnp.bfloat16), 'seq', scatter_dimension...  21.7 us
    reduce_scatter x1, waiting for transfers between devices, per_device(): lax.psum_scatter(full_values.astype(jnp.bfloat16), 'seq', scatter_dimensi...  16.7 us
    ppermute x3, waiting for transfers between devices, per_device(): lax.ppermute(ring[-1], 'seq', [(dev, (dev + 1) % 4) for dev in range(4)])  14.2 us
    unnamed x22, local copies, waits for them, and re-layouts  7.71 us
    dot_general x2, matrix products, contract_last(): lax.dot_general(left, right, (((1,), (1,)), ((), ())), preferred_element_...  5.85 us
    all_to_all x1, starting transfers between devices, owner_blocks(): lax.all_to_all(key_part.astype(jnp.bfloat16), 'head', split_axis=0, conca...  5.51 us
    all_to_all x1, starting transfers between devices, owner_blocks(): lax.all_to_all(value_part.astype(jnp.bfloat16), 'head', split_axis=0, con...  5.51 us
    all_to_all x1, waiting for transfers between devices, owner_blocks(): lax.all_to_all(key_part.astype(jnp.bfloat16), 'head', split_axis=0, conca...  5.07 us
  transfers between devices with their start and end apart: 9, of which 7 were waited for; matrix products, arithmetic and copies ran while one was open for 24% of the time, Pallas kernels for 0%

profile of v1, /device:TPU:0, one launch (start us, length us, event | category | flops | bytes accessed | tf_op | source)
XLA Modules:
  0.0 124.7 jit_solution(7170528504019792830)
XLA Ops:
  7.2 0.0 copy-start
  7.2 0.0 all-gather.5.cloned.1.call-start
  7.2 0.7 all-gather.5.cloned.1.call-update
  7.9 0.0 all-gather.7.cloned.1.call-start
  8.0 0.7 all-gather.7.cloned.1.call-update
  8.7 0.0 reduce-scatter.5.cloned.1.call-start
  8.7 0.5 collective-permute-start
  9.3 0.7 select_reduce_fusion.1
  10.0 5.4 %collective-permute-done = bf16[512,256]{1,0:T(8,128)(2,1)S(1)} collective-permute-done((bf16[512,256]{1,0:T(8,128)(2,1)}, bf16[512,256]{1,0:T(8,128)(2,1)S(1)}, u32[]{:S(2)}, u32[]{:S(2)}) %collective-permute-start) | collective-permute-done | bytes 262176 | tf_op jit(solution)/shard_map/ppermute | solution.py:105
  15.5 0.0 collective-permute-start.1
  15.5 0.7 select_reduce_fusion
  16.3 0.8 reduce-window_clone.1
  17.1 4.2 %collective-permute-done.1 = bf16[512,256]{1,0:T(8,128)(2,1)S(1)} collective-permute-done((bf16[512,256]{1,0:T(8,128)(2,1)S(1)}, bf16[512,256]{1,0:T(8,128)(2,1)S(1)}, u32[]{:S(2)}, u32[]{:S(2)}) %collective-permute-start.1) | collective-permute-done | bytes 262176 | tf_op jit(solution)/shard_map/ppermute | solution.py:105
  21.3 2.5 %collective-permute-start.2 = (bf16[512,256]{1,0:T(8,128)(2,1)S(1)}, bf16[512,256]{1,0:T(8,128)(2,1)S(1)}, u32[]{:S(2)}, u32[]{:S(2)}) collective-permute-start(bf16[512,256]{1,0:T(8,128)(2,1)S(1)} %collective-permute-done.1), channel_id=1, source_target_pairs={{0,8},{8,16},{16,24},{24,0},{1,9},{9,17},{17,25},{25,1},{2,10},{10... | collective-permute-start | bytes 786440 | tf_op jit(solution)/shard_map/ppermute | solution.py:105
  23.8 0.7 subtract_bitcast_fusion
  24.5 1.1 copy.11
  25.6 0.1 convert_reduce_fusion.3
  25.7 0.1 convert_reduce_fusion.2
  25.7 4.6 %collective-permute-done.2 = bf16[512,256]{1,0:T(8,128)(2,1)S(1)} collective-permute-done((bf16[512,256]{1,0:T(8,128)(2,1)S(1)}, bf16[512,256]{1,0:T(8,128)(2,1)S(1)}, u32[]{:S(2)}, u32[]{:S(2)}) %collective-permute-start.2) | collective-permute-done | bytes 262176 | tf_op jit(solution)/shard_map/ppermute | solution.py:105
  30.3 0.7 constant_dynamic-update-slice_fusion.7
  31.0 0.7 constant_dynamic-update-slice_fusion.6
  31.7 0.7 constant_dynamic-update-slice_fusion.5
  32.5 2.6 %fusion.1 = (f32[512]{0:T(512)S(1)}, f32[512,2048]{1,0:T(8,128)S(1)}) fusion(s32[512]{0:T(512)S(1)} %fusion.46, s32[2048]{0:T(1024)S(1)} %fusion.44, s32[2048]{0:T(1024)S(1)} %convert_reduce_fusion.2, s32[512]{0:T(512)S(1)} %convert_reduce_fusion.3, bf16[1,2048,256]{2,1,0:T(8,128)(2,1)} %all-gather.5.cloned.1.call-done, bf16[1,512,256]{2,1,0:T(8,128)(2,1)S(1)} %copy-done), kind=kOutput, calls=%fused_computation.6 | convolution fusion | flops 543161856 | bytes 5527552 | tf_op jit(solution)/shard_map/dot_general | solution.py:11
  35.0 0.0 copy-start.4
  35.1 1.7 %fusion.5 = f32[512]{0:T(512)S(1)} fusion(f32[512,2048]{1,0:T(8,128)S(1)} %get-tuple-element.4, f32[512]{0:T(512)S(1)} %broadcast_maximum_fusion, s32[512]{0:T(512)S(1)} %fusion.46, s32[2048]{0:T(1024)S(1)} %fusion.44, s32[2048]{0:T(1024)S(1)} %convert_reduce_fusion.2, s32[512]{0:T(512)S(1)} %convert_reduce_fusion.3), kind=kLoop, calls=%fused_computation.12 | loop fusion | flops 8388096 | bytes 4218880 | tf_op jit(solution)/shard_map/reduce_sum | solution.py:97
  36.8 0.2 copy-done.1
  37.0 3.0 %convolution_convert_fusion = bf16[2048,256]{1,0:T(8,128)(2,1)} fusion(f32[512,2048]{1,0:T(8,128)S(1)} %get-tuple-element.4, f32[512]{0:T(512)S(1)} %log_add_fusion, bf16[1,512,256]{2,1,0:T(8,128)(2,1)S(1)} %copy-done.4, s32[2048]{0:T(1024)S(1)} %fusion.44, s32[2048]{0:T(1024)S(1)} %convert_reduce_fusion.2, s32[512]{0:T(512)S(1)} %fusion.46, ...), kind=kOutput, calls=%fused_computation.10 | convolution fusion | flops 544735232 | bytes 5527552 | tf_op jit(solution)/shard_map/dot_general | solution.py:17
  40.0 0.0 reduce-scatter.5.cloned.1.call-update
  40.0 0.0 reduce-scatter.3.cloned.1.call-start
  40.0 0.7 constant_dynamic-update-slice_fusion.4
  40.8 0.7 constant_dynamic-update-slice_fusion.3
  41.5 0.7 constant_dynamic-update-slice_fusion.2
  42.2 0.7 constant_dynamic-update-slice_fusion.1
  43.0 0.7 constant_dynamic-update-slice_fusion
  43.7 5.0 %all-gather.7.cloned.1.call-done = bf16[1,2048,256]{2,1,0:T(8,128)(2,1)} async-done(((bf16[1,512,256]{2,1,0:T(8,128)(2,1)}), bf16[1,2048,256]{2,1,0:T(8,128)(2,1)}) %all-gather.7.cloned.1.call-update) | async-done | bytes 1048592 | tf_op jit(solution)/shard_map/all_gather | solution.py:91
  48.7 4.2 %fusion.29 = f32[512]{0:T(512)S(1)} fusion(bf16[1,2048,256]{2,1,0:T(8,128)(2,1)} %all-gather.7.cloned.1.call-done, f32[512,2048]{1,0:T(8,128)} %copy-done.1, f32[512]{0:T(512)S(1)} %broadcast_maximum_fusion, bf16[1,512,256]{1,2,0:T(8,128)(2,1)S(1)} %copy.11, f32[512]{0:T(512)S(1)} %fusion.5, s32[2048]{0:T(1024)S(1)} %fusion.44, ...), kind=kOutput, calls=%fused_computation.27 | convolution fusion | flops 545783296 | bytes 5531648 | tf_op jit(solution)/shard_map/dot_general | solution.py:98
  52.9 3.3 %fusion = bf16[512,2048]{1,0:T(8,128)(2,1)S(1)} fusion(f32[512,2048]{1,0:T(8,128)S(1)} %copy-done.2, f32[512]{0:T(512)S(1)} %fusion.29, f32[512]{0:T(512)S(1)} %log_add_fusion, bf16[4096,256]{1,0:T(8,128)(2,1)} %constant_dynamic-update-slice_fusion, s32[]{:T(128)S(6)} %select_n.94, bf16[1,512,256]{2,1,0:T(8,128)(2,1)S(1)} %copy-done.4, s32[512]{0:T(512)S(1)} %fusion.46, ...), kind=kOutput, calls=%fused_computation.1 | convolution fusion | flops 546308096 | bytes 7626756 | tf_op jit(solution)/shard_map/dot_general | solution.py:11
  56.2 1.3 %copy-done.6 = bf16[512,2048]{1,0:T(8,128)(2,1)} copy-done((bf16[512,2048]{1,0:T(8,128)(2,1)}, bf16[512,2048]{1,0:T(8,128)(2,1)S(1)}, u32[]{:S(2)}) %copy-start.6) | copy-done | bytes 2097176
  57.5 1.7 %fusion.3 = bf16[2048,256]{1,0:T(8,128)(2,1)} fusion(bf16[512,2048]{1,0:T(8,128)(2,1)S(1)} %fusion, bf16[1,512,256]{2,1,0:T(8,128)(2,1)S(1)} %copy-done), kind=kOutput, calls=%fused_computation.9 | convolution fusion | flops 537919488 | bytes 3407872 | tf_op jit(solution)/shard_map/dot_general | solution.py:17
  59.3 0.0 reduce-scatter.3.cloned.1.call-update
  59.3 16.7 %reduce-scatter.5.cloned.1.call-done = bf16[512,256]{1,0:T(8,128)(2,1)} async-done(((bf16[2048,256]{1,0:T(8,128)(2,1)}), bf16[512,256]{1,0:T(8,128)(2,1)}) %reduce-scatter.5.cloned.1.call-update) | async-done | bytes 262160 | tf_op jit(solution)/shard_map/reduce_scatter | solution.py:121
  76.0 5.5 %all-to-all-start.1 = ((bf16[8,64,256]{2,1,0:T(8,128)(2,1)}), bf16[8,64,256]{2,1,0:T(8,128)(2,1)S(1)}, u32[]{:S(2)}, u32[]{:S(2)}) async-start(bf16[8,64,256]{2,1,0:T(8,128)(2,1)} %bitcast.49), calls=%async_computation.3 | async-start | bytes 524288 | tf_op jit(solution)/shard_map/all_to_all | solution.py:42
  81.6 21.7 %reduce-scatter.3.cloned.1.call-done = bf16[512,256]{1,0:T(8,128)(2,1)} async-done(((bf16[2048,256]{1,0:T(8,128)(2,1)}), bf16[512,256]{1,0:T(8,128)(2,1)}) %reduce-scatter.3.cloned.1.call-update) | async-done | bytes 262160 | tf_op jit(solution)/shard_map/reduce_scatter | solution.py:118
  103.3 5.5 %all-to-all-start = ((bf16[8,64,256]{2,1,0:T(8,128)(2,1)}), bf16[8,64,256]{2,1,0:T(8,128)(2,1)S(1)}, u32[]{:S(2)}, u32[]{:S(2)}) async-start(bf16[8,64,256]{2,1,0:T(8,128)(2,1)} %bitcast.50), calls=%async_computation.1 | async-start | bytes 524288 | tf_op jit(solution)/shard_map/all_to_all | solution.py:39
  108.8 3.0 %fusion.13 = bf16[1,512,256]{2,1,0:T(8,128)(2,1)} fusion(bf16[512,2048]{1,0:T(8,128)(2,1)} %copy-done.6, bf16[1,2048,256]{2,1,0:T(8,128)(2,1)S(1)} %copy-done.5), kind=kOutput, calls=%fused_computation.19 | convolution fusion | flops 537133056 | bytes 3407872 | tf_op jit(solution)/shard_map/dot_general | solution.py:28
  111.8 0.7 convert_reduce_fusion
  112.5 5.1 %all-to-all-done = bf16[8,64,256]{2,1,0:T(8,128)(2,1)S(1)} async-done(((bf16[8,64,256]{2,1,0:T(8,128)(2,1)}), bf16[8,64,256]{2,1,0:T(8,128)(2,1)S(1)}, u32[]{:S(2)}, u32[]{:S(2)}) %all-to-all-start) | async-done | bytes 262176 | tf_op jit(solution)/shard_map/all_to_all | solution.py:39
  117.5 0.7 convert_reduce_fusion.1
  (18 shorter events, 0.1 us)
Async XLA Ops:
  7.2 25.3 %copy-start = (bf16[1,512,256]{2,1,0:T(8,128)(2,1)S(1)}, bf16[1,512,256]{2,1,0:T(8,128)(2,1)}, u32[]{:S(2)}) copy-start(bf16[1,512,256]{2,1,0:T(8,128)(2,1)} %param.6) | copy-start | bytes 786436
  7.2 25.3 %all-gather.5.cloned.1.call-start = ((), (), s32[]{:S(2)}) async-start(), calls=%async_computation.6 | async-start | bytes 1310720 | tf_op jit(solution)/shard_map/all_gather | solution.py:102
  7.9 40.8 %all-gather.7.cloned.1.call-start = ((), (), s32[]{:S(2)}) async-start(), calls=%async_computation.7 | async-start | bytes 1310720 | tf_op jit(solution)/shard_map/all_gather | solution.py:91
  8.7 67.4 %reduce-scatter.5.cloned.1.call-start = ((), (), s32[]{:S(2)}) async-start(), calls=%async_computation.5 | async-start | bytes 1310720 | tf_op jit(solution)/shard_map/reduce_scatter | solution.py:121
  8.7 6.8 %collective-permute-start = (bf16[512,256]{1,0:T(8,128)(2,1)}, bf16[512,256]{1,0:T(8,128)(2,1)S(1)}, u32[]{:S(2)}, u32[]{:S(2)}) collective-permute-start(bf16[512,256]{1,0:T(8,128)(2,1)} %bitcast.48), channel_id=1, source_target_pairs={{0,8},{8,16},{16,24},{24,0},{1,9},{9,17},{17,25},{25,1},{2,10},{10... | collective-permute-start | bytes 786440 | tf_op jit(solution)/shard_map/ppermute | solution.py:105
  15.5 5.8 %collective-permute-start.1 = (bf16[512,256]{1,0:T(8,128)(2,1)S(1)}, bf16[512,256]{1,0:T(8,128)(2,1)S(1)}, u32[]{:S(2)}, u32[]{:S(2)}) collective-permute-start(bf16[512,256]{1,0:T(8,128)(2,1)S(1)} %collective-permute-done), channel_id=1, source_target_pairs={{0,8},{8,16},{16,24},{24,0},{1,9},{9,17},{17,25},{25,1},{2,10},{10... | collective-permute-start | bytes 786440 | tf_op jit(solution)/shard_map/ppermute | solution.py:105
  21.3 9.1 %collective-permute-start.2 = (bf16[512,256]{1,0:T(8,128)(2,1)S(1)}, bf16[512,256]{1,0:T(8,128)(2,1)S(1)}, u32[]{:S(2)}, u32[]{:S(2)}) collective-permute-start(bf16[512,256]{1,0:T(8,128)(2,1)S(1)} %collective-permute-done.1), channel_id=1, source_target_pairs={{0,8},{8,16},{16,24},{24,0},{1,9},{9,17},{17,25},{25,1},{2,10},{10... | collective-permute-start | bytes 786440 | tf_op jit(solution)/shard_map/ppermute | solution.py:105
  35.0 1.9 %copy-start.1 = (f32[512,2048]{1,0:T(8,128)}, f32[512,2048]{1,0:T(8,128)S(1)}, u32[]{:S(2)}) copy-start(f32[512,2048]{1,0:T(8,128)S(1)} %get-tuple-element.4) | copy-start | bytes 12582916
  35.0 1.9 %copy-start.4 = (bf16[1,512,256]{2,1,0:T(8,128)(2,1)S(1)}, bf16[1,512,256]{2,1,0:T(8,128)(2,1)}, u32[]{:S(2)}) copy-start(bf16[1,512,256]{2,1,0:T(8,128)(2,1)} %param.9) | copy-start | bytes 786436
  37.0 3.1 %copy-start.3 = (bf16[1,512,256]{2,1,0:T(8,128)(2,1)S(1)}, bf16[1,512,256]{2,1,0:T(8,128)(2,1)}, u32[]{:S(2)}) copy-start(bf16[1,512,256]{2,1,0:T(8,128)(2,1)} %param.8) | copy-start | bytes 786436
  40.0 63.3 %reduce-scatter.3.cloned.1.call-start = ((), (), s32[]{:S(2)}) async-start(), calls=%async_computation.4 | async-start | bytes 1310720 | tf_op jit(solution)/shard_map/reduce_scatter | solution.py:118
  48.7 4.2 %copy-start.2 = (f32[512,2048]{1,0:T(8,128)S(1)}, f32[512,2048]{1,0:T(8,128)}, u32[]{:S(2)}) copy-start(f32[512,2048]{1,0:T(8,128)} %copy-done.1) | copy-start | bytes 12582916
  56.2 1.4 %copy-start.6 = (bf16[512,2048]{1,0:T(8,128)(2,1)}, bf16[512,2048]{1,0:T(8,128)(2,1)S(1)}, u32[]{:S(2)}) copy-start(bf16[512,2048]{1,0:T(8,128)(2,1)S(1)} %fusion) | copy-start | bytes 6291460
  57.5 51.3 %copy-start.5 = (bf16[1,2048,256]{2,1,0:T(8,128)(2,1)S(1)}, bf16[1,2048,256]{2,1,0:T(8,128)(2,1)}, u32[]{:S(2)}) copy-start(bf16[1,2048,256]{2,1,0:T(8,128)(2,1)} %all-gather.5.cloned.1.call-done) | copy-start | bytes 3145732
  76.0 27.2 %all-to-all-start.1 = ((bf16[8,64,256]{2,1,0:T(8,128)(2,1)}), bf16[8,64,256]{2,1,0:T(8,128)(2,1)S(1)}, u32[]{:S(2)}, u32[]{:S(2)}) async-start(bf16[8,64,256]{2,1,0:T(8,128)(2,1)} %bitcast.49), calls=%async_computation.3 | async-start | bytes 524288 | tf_op jit(solution)/shard_map/all_to_all | solution.py:42
  103.3 14.3 %all-to-all-start = ((bf16[8,64,256]{2,1,0:T(8,128)(2,1)}), bf16[8,64,256]{2,1,0:T(8,128)(2,1)S(1)}, u32[]{:S(2)}, u32[]{:S(2)}) async-start(bf16[8,64,256]{2,1,0:T(8,128)(2,1)} %bitcast.50), calls=%async_computation.1 | async-start | bytes 524288 | tf_op jit(solution)/shard_map/all_to_all | solution.py:39
Sparse Core Ops, SparseCore 0:
  9.5 21.1 all-gather.4
  32.3 16.3 all-gather.6
  51.2 24.7 reduce-scatter.4
  78.4 24.8 reduce-scatter.2
